TPU v7x, 128 devices: a whole 4x4x4 slice. The times are simulated.
128 devices in a mesh: lat: 8 (over y, core), lon: 16 (over x, z).
Axes of the slice: x: 4, y: 4, z: 4, core: 2. Of those that a mesh axis runs over, the one named last changes fastest.
Arguments:
- obs_pert: bfloat16 [4096, 512, 256], P(('lat', 'lon')), may hold values from -3 to 3
- obs_weight: bfloat16 [4096, 512], P(('lat', 'lon')), may hold values from 0.5 to 2
- innovation: bfloat16 [4096, 512], P(('lat', 'lon')), may hold values from -6 to 6
- batch_len: int32 [128, 32], P(('lat', 'lon')), may hold values from 1 to 512, 10240 in all within a row
- batch_owner: int32 [4096, 1], P(('lat', 'lon')), may hold values from 0 to 15; in each aligned block of 32 rows (0 to 31, 32 to 63, ...) at most 4 rows name the same one
- batch_points: int32 [4096, 3], P(('lat', 'lon')), may hold values from 0 to 7, all different within a row
- batch_count: int32 [4096], P(('lat', 'lon')), may hold values from 1 to 3
- batch_taper: bfloat16 [4096, 3], P(('lat', 'lon')), may hold values from 0.25 to 1
- background: bfloat16 [64, 2048, 256], P('lat', 'lon'), may hold values from -6 to 6
- stencil: int32 [2, 64, 2048], P(None, 'lat', 'lon'), may hold values from 0 to 63, as said below
- frac: float32 [2, 64, 2048], P(None, 'lat', 'lon'), may hold values from 0 to 1
Outputs:
- analysis: bfloat16 [64, 2048, 256], P('lat', 'lon')
Inputs may be any that keep to these rules, and one draw needn't show every extreme that they name: `batch_owner`: among the 32 batches held by one device, at most 4 share an owner, and in every draw some owner has exactly 4 of them. `batch_points`: the entries of a row are distinct; local point p of an owner is its point p // 4 along latitude and p % 4 along longitude. Only the first batch_count entries of a batch's row of batch_points and batch_taper count. `batch_len`: each row sums to 10240 and its largest entry is 512. For a cell in the block of cells a * 8 .. (a + 1) * 8 - 1 along latitude and c * 128 .. (c + 1) * 128 - 1 along longitude, stencil[0] lies in a * 2 - 1 .. (a + 1) * 2 - 1 and in 0 .. 14, and stencil[1] is (c * 4 - 1 + t) mod 64 for some t in 0 .. 4.
All inputs are finite; a program needn't handle non-finite values.
Results may differ from a plain program's by a relative error of at most 0.0059.
Values may be sent and summed in bfloat16 or wider, within the bound.
A program may use at most 128 MiB of HBM per device.

v0:
```python
import jax
import jax.numpy as jnp
from jax import lax
from jax.experimental import pallas as pl
from jax.experimental.pallas import tpu as pltpu
from jax.sharding import PartitionSpec as P

MEMBERS = 256
NOBS = 512
BAT = 32
TOP = 3
PTS = 8
ITERS = 6
HALF = 128
MESH = pl.DeviceIdType.MESH
F32 = jnp.float32
BF16 = jnp.bfloat16
COPIES = 64


def iota(shape, dim):
    return lax.broadcasted_iota(jnp.int32, shape, dim)


def dot(a, b):
    return jnp.dot(a, b, preferred_element_type=F32)


def dot_first(a, b):
    return lax.dot_general(a, b, (((0,), (0,)), ((), ())), preferred_element_type=F32)


def relative_bits(owner, me):
    ox, oz, mx, mz = owner // 4, owner % 4, me // 4, me % 4
    gx = (ox ^ (ox >> 1)) ^ (mx ^ (mx >> 1))
    gz = (oz ^ (oz >> 1)) ^ (mz ^ (mz >> 1))
    return (gx & 1, gx >> 1, gz & 1, gz >> 1)


def moments_kernel(
    owner_s,
    points_s,
    count_s,
    len_s,
    weight_ref,
    innov_ref,
    taper_ref,
    pert_hbm,
    packed_ref,
    extra_ref,
    coef_ref,
    pert,
    wide_w,
    wide_i,
    acc,
    extra_f,
    rows_i,
    used_s,
    pos_s,
    sems,
):
    me = lax.axis_index("lon")

    def fetch(b, part):
        rows = pl.ds(part * 256, 256)
        return pltpu.make_async_copy(pert_hbm.at[b, rows], pert.at[b, rows], sems.at[part, b])

    def start(b, carry):
        fetch(b, 0).start()

        @pl.when(len_s[0, b] > 256)
        def _():
            fetch(b, 1).start()

        return carry

    lax.fori_loop(0, BAT, start, 0)

    packed_ref[...] = jnp.zeros(packed_ref.shape, BF16)
    extra_f[...] = jnp.zeros(extra_f.shape, F32)
    wide_w[...] = weight_ref[...].astype(F32)
    wide_i[...] = innov_ref[...].astype(F32)
    for o in range(16):
        used_s[o] = 0

    def place(b, carry):
        owner = owner_s[b, 0]
        rank = used_s[owner]
        used_s[owner] = rank + 1
        bits = relative_bits(owner, me)
        for k in range(4):
            d = [bits[(k + i) % 4] for i in range(4)]
            pos_s[k, b] = d[0] * 8 + d[1] * 4 + d[2] * 2 + d[3]
        pos_s[4, b] = rank
        full = lambda v: jnp.full((1, HALF), v, jnp.int32)
        rows_i[0, pl.ds(b, 1), :] = full(owner * 4 + rank)
        rows_i[1, pl.ds(b, 1), :] = full(count_s[b])
        for j in range(TOP):
            rows_i[2 + j, pl.ds(b, 1), :] = full(points_s[b, j])
        return carry

    lax.fori_loop(0, BAT, place, 0)

    lane = iota((BAT, HALF), 1)
    taper = taper_ref[...].astype(F32)
    coef = jnp.zeros((BAT, HALF), F32)
    for j in range(TOP):
        hit = (rows_i[2 + j] == lane) & (rows_i[1] > j)
        coef = coef + jnp.where(hit, taper[:, j : j + 1], 0.0)
    spot = jnp.where(rows_i[0] == lane, 1.0, 0.0)
    coef_ref[...] = dot_first(coef.astype(BF16), spot.astype(BF16))[0:PTS, :]

    row, col = iota((HALF, HALF), 0), iota((HALF, HALF), 1)
    first = iota((16, 256), 0)

    def product(b, part, length):
        p = pert[b, part * 256 : part * 256 + 256, :]
        cols = slice(part * 256, part * 256 + 256)
        live = (iota((1, 256), 1) + part * 256) < length
        w = jnp.where(live, wide_w[pl.ds(b, 1), cols], 0.0)
        wi = w * wide_i[pl.ds(b, 1), cols]
        high = wi.astype(BF16).astype(F32)
        low = wi - high
        tail = jnp.where(first == 0, high, jnp.where(first == 1, low, 0.0)).astype(BF16)
        scaled = (p.T.astype(F32) * w).astype(BF16)
        return dot(jnp.concatenate([scaled, tail], axis=0), p)

    def one(b, carry):
        length = len_s[0, b]
        fetch(b, 0).wait()
        acc[...] = product(b, 0, length)

        @pl.when(length > 256)
        def _():
            fetch(b, 1).wait()
            acc[...] += product(b, 1, length)

        corner = acc[HALF:256, HALF:256]
        left = jnp.where(col >= row, acc[0:HALF, 0:HALF], corner)
        top = jnp.concatenate([left, acc[0:HALF, HALF:256]], axis=1).astype(BF16)
        rank = pos_s[4, b]
        for k in range(4):
            for rc in range(2):
                at = 32 * k + 16 * rc
                packed_ref[k, pos_s[k, b], rc, rank] = top[at : at + 16, :]
        proj = acc[256:257, :] + acc[257:258, :]
        base = pos_s[0, b] * 16 + rank * 4
        extra_f[pl.ds(base, 1), :] = jnp.sum(
            jnp.where(col == row, corner, 0.0), axis=0, keepdims=True
        )
        extra_f[pl.ds(base + 1, 1), :] = proj[:, 0:HALF]
        extra_f[pl.ds(base + 2, 1), :] = proj[:, HALF:256]
        return carry

    lax.fori_loop(0, BAT, one, 0)
    extra_ref[...] = extra_f[...].astype(BF16).reshape(extra_ref.shape)


def moments(obs_pert, obs_weight, innovation, batch_len, owner, points, count, taper):
    smem = pl.BlockSpec(memory_space=pltpu.SMEM)
    vmem = pl.BlockSpec(memory_space=pltpu.VMEM)
    return pl.pallas_call(
        moments_kernel,
        out_shape=(
            jax.ShapeDtypeStruct((4, 16, 2, 4, 16, 256), BF16),
            jax.ShapeDtypeStruct((16, 16, HALF), BF16),
            jax.ShapeDtypeStruct((PTS, HALF), F32),
        ),
        in_specs=[smem, smem, smem, smem, vmem, vmem, vmem, pl.BlockSpec(memory_space=pl.ANY)],
        out_specs=(vmem, vmem, vmem),
        scratch_shapes=[
            pltpu.VMEM((BAT, NOBS, MEMBERS), BF16),
            pltpu.VMEM((BAT, NOBS), F32),
            pltpu.VMEM((BAT, NOBS), F32),
            pltpu.VMEM((272, 256), F32),
            pltpu.VMEM((256, HALF), F32),
            pltpu.VMEM((5, BAT, HALF), jnp.int32),
            pltpu.SMEM((16,), jnp.int32),
            pltpu.SMEM((5, BAT), jnp.int32),
            pltpu.SemaphoreType.DMA((2, BAT)),
        ],
        compiler_params=pltpu.CompilerParams(vmem_limit_bytes=40 << 20),
        name="moments",
    )(owner, points, count, batch_len, obs_weight, innovation, taper, obs_pert)


def flip(x, z, dim):
    if dim == 0:
        return x + 1 - 2 * (x % 2), z
    if dim == 1:
        return 3 - x, z
    if dim == 2:
        return x, z + 1 - 2 * (z % 2)
    return x, 3 - z


def root_iteration(e_s, eb_s, z_s, scal, k):
    new = []
    for p in range(4):
        m, z = scal[p]
        f = 1.5 - 0.5 * m
        e = e_s[p]
        eb = eb_s[p]
        if k == 0:
            z_s[p] = -0.5 * e
        else:
            r = z_s[p]
            z_s[p] = f * r - 0.5 * (dot(r.astype(BF16), eb) + z * e)
        if k < ITERS - 1:
            g = m * f
            h = (f - 0.5 * m) * e - 0.5 * dot(eb, eb)
            e_new = f * h - 0.5 * (g * e + dot(h.astype(BF16), eb))
            e_s[p] = e_new
            eb_s[p] = e_new.astype(BF16)
        new.append((m * f * f, z * f))
    return new


def exchange_kernel(
    packed,
    extra,
    coef,
    window_out,
    held,
    coef_n,
    coef_d,
    send3,
    recv3,
    send4,
    recv4,
    mine1,
    total,
    xheld,
    xsend3,
    xrecv3,
    xsend4,
    xrecv4,
    xmine1,
    xtotal,
    e_s,
    eb_s,
    z_s,
    window,
    local_sems,
    out_sems,
    send_sems,
    recv_sems,
):
    lat, lon = lax.axis_index("lat"), lax.axis_index("lon")
    x, z = lon // 4, lon % 4

    def to(dim):
        hx, hz = flip(x, z, dim % 4)
        return (lat, hx * 4 + hz)

    east, west = (lat, (lon + 1) % 16), (lat, (lon + 15) % 16)
    south, north = ((lat + 1) % 8, lon), ((lat + 7) % 8, lon)

    barrier = pltpu.get_barrier_semaphore()
    peers = [to(d) for d in range(4)] + [east, west, south, north]
    for peer in peers:
        pl.semaphore_signal(barrier, inc=1, device_id=peer, device_id_type=MESH)
    own = [
        pltpu.make_async_copy(packed.at[k, 0:8], held.at[k, :, :, 0], local_sems.at[k])
        for k in range(4)
    ]
    own.append(pltpu.make_async_copy(extra.at[0:8], xheld.at[:, 0], local_sems.at[4]))
    for c in own:
        c.start()
    pl.semaphore_wait(barrier, len(peers))

    used = []

    def push(src, dst, peer):
        n = len(used)
        c = pltpu.make_async_remote_copy(
            src_ref=src,
            dst_ref=dst,
            send_sem=send_sems.at[n],
            recv_sem=recv_sems.at[n],
            device_id=peer,
            device_id_type=MESH,
        )
        c.start()
        used.append(c)
        return c

    cn = [push(coef, coef_n.at[k], to(k)) for k in range(4)]
    s1a = [push(packed.at[k, 12:16], held.at[k, 4:8, :, 1], to(k)) for k in range(4)]
    x1 = push(extra.at[8:16], xheld.at[:, 1], to(0))
    s1b = [push(packed.at[k, 8:12], held.at[k, 0:4, :, 1], to(k)) for k in range(4)]

    for c in own:
        c.wait()
    for k in range(4):
        cn[k].wait_recv()
    cd = [push(coef_n.at[k], coef_d.at[k], to(k + 1)) for k in range(4)]
    s2a, s2b = [], []
    for k in range(4):
        s1a[k].wait_recv()
        s2a.append(push(held.at[k, 6:8, :, 0:2], held.at[k, 2:4, :, 2:4], to(k + 1)))
    for k in range(4):
        s2b.append(push(held.at[k, 4:6, :, 0:2], held.at[k, 0:2, :, 2:4], to(k + 1)))
    x1.wait_recv()
    x2 = push(xheld.at[4:8, 0:2], xheld.at[0:4, 2:4], to(1))

    def sources(k):
        rows = [coef[...], coef_n[k], coef_n[(k + 1) % 4], coef_d[k]]
        return jnp.concatenate(rows, axis=0).astype(BF16)

    def served(k, pos):
        sx, sz = x, z
        if pos & 2:
            sx, sz = flip(sx, sz, (k + 2) % 4)
        if pos & 1:
            sx, sz = flip(sx, sz, (k + 3) % 4)
        return sx * 4 + sz

    def spread(k, pos, width, each):
        lane = iota((HALF, width), 1)
        pick = jnp.where(
            iota((HALF, width), 0) == served(k, pos) * 4 + (lane // each) % 4, 1.0, 0.0
        ).astype(BF16)
        every = dot(sources(k), pick)
        lane8 = iota((8, width), 1) // (4 * each)
        out = jnp.zeros((8, width), F32)
        for j in range(4):
            out = out + jnp.where(lane8 == j, every[8 * j : 8 * j + 8, :], 0.0)
        return out

    def expand(weights, rows, each):
        width = weights.shape[1]
        keep = iota((rows, width), 1) % each == iota((rows, width), 0)
        blocks = [
            jnp.where(keep, jnp.broadcast_to(weights[p : p + 1, :], (rows, width)), 0.0)
            for p in range(PTS)
        ]
        return jnp.concatenate(blocks, axis=0).astype(BF16)

    def merged(k, pos):
        lhs = expand(spread(k, pos, 256, 16), 16, 16)
        return [
            dot(lhs, held[k, pos, rc].reshape(256, 256)).reshape(PTS, 16, 256) for rc in range(2)
        ]

    def xmerged(pos):
        lhs = expand(spread(0, pos, HALF, 4), 8, 4)
        return dot(lhs[:, 0:64], xheld[pos].reshape(64, HALF))

    s3a, s3b = [], []
    for k in range(4):
        cd[k].wait_recv()
        s1b[k].wait_recv()
    for pos in (3, 2):
        for k in range(4):
            if pos == 3:
                s2a[k].wait_recv()
            for rc, value in enumerate(merged(k, pos)):
                send3[k, pos - 2, :, 16 * rc : 16 * rc + 16, :] = value.astype(BF16)
            if pos == 3:
                s3a.append(push(send3.at[k, 1], recv3.at[k, 1], to(k + 2)))
            else:
                for h in range(2):
                    span = pl.ds(4 * h, 4)
                    s3b.append(push(send3.at[k, 0, span], recv3.at[k, 0, span], to(k + 2)))
    x2.wait_recv()
    for pos in (3, 2):
        xsend3[pos - 2] = xmerged(pos).astype(BF16)
    x3 = push(xsend3, xrecv3, to(2))

    for pos in (1, 0):
        for k in range(4):
            if pos == 1:
                s2b[k].wait_recv()
            for rc, value in enumerate(merged(k, pos)):
                if pos == 1:
                    mine1[k, :, 16 * rc : 16 * rc + 16, :] = value
                else:
                    at = 32 * k + 16 * rc
                    total[:, at : at + 16, :] = value
    xmine1[...] = xmerged(1)
    xtotal[...] = xmerged(0)

    s4 = []
    for k in range(4):
        s3a[k].wait_recv()
        send4[k] = (mine1[k] + recv3[k, 1].astype(F32)).astype(BF16)
        s4.append(push(send4.at[k, 0:4], recv4.at[k, 0:4], to(k + 3)))
    x3.wait_recv()
    xsend4[...] = (xmine1[...] + xrecv3[1].astype(F32)).astype(BF16)
    x4 = push(xsend4, xrecv4, to(3))
    for k in range(4):
        s4.append(push(send4.at[k, 4:8], recv4.at[k, 4:8], to(k + 3)))
    x4.wait_recv()
    xtotal[...] += xrecv3[0].astype(F32) + xrecv4[...].astype(F32)

    row, col = iota((HALF, HALF), 0), iota((HALF, HALF), 1)
    outs = []

    def keep(n):
        c = pltpu.make_async_copy(window.at[n], window_out.at[n], out_sems.at[n])
        c.start()
        outs.append(c)

    side = []
    for h in range(2):
        scal, scales = [], []
        for k in range(4):
            s3b[2 * k + h].wait_recv()
            s4[4 * h + k].wait_recv()
        for i in range(4):
            p = 4 * h + i
            for k in range(4):
                total[p, 32 * k : 32 * k + 32, :] += recv3[k, 0, p].astype(F32) + recv4[
                    k, p
                ].astype(F32)
            left, right = total[p, :, 0:HALF], total[p, :, HALF:256]
            turned = left.T
            eye = jnp.where(row == col, float(MEMBERS - 1), 0.0)
            a = jnp.where(col >= row, left, turned) + eye
            c = jnp.where(col < row, left, turned)
            c = jnp.where(col == row, xtotal[8 * p : 8 * p + 1, :], c) + eye
            square = jnp.sum(a * a + c * c + 2.0 * (right * right), keepdims=True)
            trace = jnp.sum(jnp.where(row == col, a + c, 0.0), keepdims=True)
            scale = jnp.sqrt(square)
            inverse = 1.0 / scale
            mean = trace * (1.0 / MEMBERS)
            off = jnp.where(row == col, mean, 0.0)
            a, c, b = (a - off) * inverse, (c - off) * inverse, right * inverse
            e_s[i] = jnp.concatenate(
                [jnp.concatenate([a, b], axis=1), jnp.concatenate([b.T, c], axis=1)], axis=0
            )
            eb_s[i] = e_s[i].astype(BF16)
            scal.append((mean * inverse, jnp.ones((1, 1), F32)))
            scales.append(scale)
        for k in range(ITERS):
            scal = root_iteration(e_s, eb_s, z_s, scal, k)
        for i in range(4):
            p = 4 * h + i
            zd = scal[i][1]
            r = z_s[i]
            high = r.astype(BF16)
            low = (r - high.astype(F32)).astype(BF16)

            def apply(v):
                vh = v.astype(BF16).astype(F32)
                first = iota((16, 256), 0)
                both = jnp.where(first == 0, vh, jnp.where(first == 1, v - vh, 0.0)).astype(BF16)
                w = dot(both, high) + dot(both, low)
                return zd * v + w[0:1, :] + w[1:2, :]

            shift = jnp.concatenate(
                [xtotal[8 * p + 1 : 8 * p + 2, :], xtotal[8 * p + 2 : 8 * p + 3, :]], axis=1
            )
            mw = apply(apply(shift)) / scales[i]
            amp = jnp.sqrt(float(MEMBERS - 1) / scales[i])
            big = iota((256, 256), 0) == iota((256, 256), 1)
            full = amp * (r + jnp.where(big, zd, 0.0)) + mw
            slot = (h + 1) * 6 + i + 1
            window[slot] = full.astype(BF16)
            if i == 0:
                side.append(push(window.at[slot], window.at[(h + 1) * 6 + 5], west))
            if i == 3:
                side.append(push(window.at[slot], window.at[(h + 1) * 6], east))
            if h == 0:
                push(window.at[slot], window.at[18 + i + 1], north)
            else:
                push(window.at[slot], window.at[i + 1], south)
            keep(slot)
    for h in range(2):
        for j in range(2):
            side[2 * h + j].wait_recv()
            at = (h + 1) * 6 + (5 if j == 0 else 0)
            column = 5 if j == 0 else 0
            if h == 0:
                push(window.at[at], window.at[18 + column], north)
            else:
                push(window.at[at], window.at[column], south)
            keep(at)
    done = set(id(c) for c in cn + cd + s1a + s1b + s2a + s2b + s3a + s3b + s4 + side)
    done |= set(id(c) for c in (x1, x2, x3, x4))
    for c in used:
        if id(c) not in done:
            c.wait_recv()
    for n in list(range(6)) + list(range(18, 24)):
        keep(n)
    for c in outs:
        c.wait()
    for c in used:
        c.wait_send()


def exchange(packed, extra, coef):
    vmem = pl.BlockSpec(memory_space=pltpu.VMEM)
    hbm = pl.BlockSpec(memory_space=pl.ANY)
    return pl.pallas_call(
        exchange_kernel,
        out_shape=jax.ShapeDtypeStruct((24, 256, 256), BF16),
        in_specs=[hbm, hbm, vmem],
        out_specs=hbm,
        scratch_shapes=[
            pltpu.VMEM((4, 8, 2, 4, 4, 16, 256), BF16),
            pltpu.VMEM((4, PTS, HALF), F32),
            pltpu.VMEM((4, PTS, HALF), F32),
            pltpu.VMEM((4, 2, PTS, 32, 256), BF16),
            pltpu.VMEM((4, 2, PTS, 32, 256), BF16),
            pltpu.VMEM((4, PTS, 32, 256), BF16),
            pltpu.VMEM((4, PTS, 32, 256), BF16),
            pltpu.VMEM((4, PTS, 32, 256), F32),
            pltpu.VMEM((PTS, HALF, 256), F32),
            pltpu.VMEM((8, 4, 16, HALF), BF16),
            pltpu.VMEM((2, 64, HALF), BF16),
            pltpu.VMEM((2, 64, HALF), BF16),
            pltpu.VMEM((64, HALF), BF16),
            pltpu.VMEM((64, HALF), BF16),
            pltpu.VMEM((64, HALF), F32),
            pltpu.VMEM((64, HALF), F32),
            pltpu.VMEM((4, 256, 256), F32),
            pltpu.VMEM((4, 256, 256), BF16),
            pltpu.VMEM((4, 256, 256), F32),
            pltpu.VMEM((24, 256, 256), BF16),
            pltpu.SemaphoreType.DMA((5,)),
            pltpu.SemaphoreType.DMA((24,)),
            pltpu.SemaphoreType.DMA((COPIES,)),
            pltpu.SemaphoreType.DMA((COPIES,)),
        ],
        compiler_params=pltpu.CompilerParams(
            collective_id=0, has_side_effects=True, vmem_limit_bytes=48 << 20
        ),
        name="exchange",
    )(packed, extra, coef)


def analysis_kernel(background, stencil, frac, window, out, weights, folded):
    lat, lon = lax.axis_index("lat"), lax.axis_index("lon")
    row_off = stencil[0] - (lat * 2 - 1)
    col_off = (stencil[1] - lon * 4 + 1) % 64
    corner = row_off * 6 + col_off
    fy, fx = frac[0], frac[1]
    kinds = (
        (0, (1.0 - fy) * (1.0 - fx)),
        (6, fy * (1.0 - fx)),
        (1, (1.0 - fy) * fx),
        (7, fy * fx),
    )
    for j in range(24):
        value = jnp.zeros((8, HALF), F32)
        for add, weight in kinds:
            value = value + jnp.where(corner + add == j, weight, 0.0)
        weights[j] = value
    for t in range(4):
        cells = background[2 * t : 2 * t + 2].reshape(256, 256)
        turned = cells.T.astype(F32)
        mean = jnp.sum(turned, axis=0, keepdims=True) * (1.0 / MEMBERS)
        deviation = (turned - mean).astype(BF16).astype(F32)
        mixed = jnp.zeros((256, 256), F32)
        for j in range(24):
            w = jnp.concatenate([weights[j, 2 * t : 2 * t + 1], weights[j, 2 * t + 1 : 2 * t + 2]], axis=1)
            mixed = mixed + dot(window[j], (deviation * w).astype(BF16))
        out[2 * t : 2 * t + 2] = (mixed + mean).T.astype(BF16).reshape(2, HALF, 256)


def analyse(background, stencil, frac, window):
    vmem = pl.BlockSpec(memory_space=pltpu.VMEM)
    return pl.pallas_call(
        analysis_kernel,
        out_shape=jax.ShapeDtypeStruct((8, HALF, 256), BF16),
        in_specs=[vmem] * 4,
        out_specs=vmem,
        scratch_shapes=[
            pltpu.VMEM((24, 8, HALF), F32),
            pltpu.VMEM((16, HALF), F32),
        ],
        compiler_params=pltpu.CompilerParams(vmem_limit_bytes=40 << 20),
        name="analysis",
    )(background, stencil, frac, window)


def on_device(
    obs_pert,
    obs_weight,
    innovation,
    batch_len,
    batch_owner,
    batch_points,
    batch_count,
    batch_taper,
    background,
    stencil,
    frac,
):
    packed, extra, coef = moments(
        obs_pert,
        obs_weight,
        innovation,
        batch_len,
        batch_owner,
        batch_points,
        batch_count,
        batch_taper,
    )
    window = exchange(packed, extra, coef)
    return analyse(background, stencil, frac, window)


def solution(mesh):
    return jax.shard_map(
        on_device,
        mesh=mesh,
        in_specs=(
            P(("lat", "lon"), None, None),
            P(("lat", "lon"), None),
            P(("lat", "lon"), None),
            P(("lat", "lon"), None),
            P(("lat", "lon"), None),
            P(("lat", "lon"), None),
            P(("lat", "lon")),
            P(("lat", "lon"), None),
            P("lat", "lon", None),
            P(None, "lat", "lon"),
            P(None, "lat", "lon"),
        ),
        out_specs=P("lat", "lon", None),
        check_vma=False,
    )
```

profile of v0, /device:TPU:1, one launch (start us, length us, event | category | flops | bytes accessed | tf_op | source)
XLA Modules:
  0.0 104.9 jit_solution(11569560121273668891)
XLA Ops:
  0.0 0.8 copy.14.taper_ref
  0.8 0.7 copy.12.owner_s
  1.5 0.8 copy.13.points_s
  2.3 0.0 copy-start
  2.3 3.4 %copy-done = bf16[32,512,256]{2,1,0:T(8,128)(2,1)S(1)} copy-done((bf16[32,512,256]{2,1,0:T(8,128)(2,1)S(1)}, bf16[32,512,256]{2,1,0:T(8,128)(2,1)}, u32[]{:S(2)}) %copy-start) | copy-done | bytes 8388632
  5.7 0.0 copy-start.3
  5.7 0.8 copy-done.3
  6.4 0.0 copy-start.4
  6.4 0.8 copy-done.4
  7.2 0.0 copy-start.7
  7.2 0.7 copy-done.7
  7.8 0.0 copy-start.8
  7.8 0.7 copy-done.8
  8.5 25.6 %moments.1 = (bf16[4,16,2,4,16,256]{5,4,3,2,1,0:T(8,128)(2,1)S(1)}, bf16[16,16,128]{2,1,0:T(8,128)(2,1)S(1)}, f32[8,128]{1,0:T(8,128)S(1)}) custom-call(s32[32,1]{1,0:T(8,128)S(1)} %copy.12.owner_s, s32[32,3]{1,0:T(8,128)S(1)} %copy.13.points_s, s32[32]{0:T(128)S(1)} %copy-done.7, s32[1,32]{1,0:T(1,128)S(1)} %copy-done.8, bf16[32,512]{1,0:T(8,128)(2,1)S(1)} %copy-done.3, ...), custom_call_target="tpu_custom_call" | custom-call | tf_op jit(solution)/shard_map/moments/pallas_call | solution.py:162
  34.1 0.0 copy-start.1
  34.1 1.9 %copy-done.1 = bf16[4,16,2,4,16,256]{5,4,3,2,1,0:T(8,128)(2,1)} copy-done((bf16[4,16,2,4,16,256]{5,4,3,2,1,0:T(8,128)(2,1)}, bf16[4,16,2,4,16,256]{5,4,3,2,1,0:T(8,128)(2,1)S(1)}, u32[]{:S(2)}) %copy-start.1) | copy-done | bytes 4194328
  36.0 0.0 copy-start.2
  36.0 0.0 copy-start.5
  36.0 0.0 copy-start.6
  36.0 64.1 %exchange.1.window = bf16[24,256,256]{2,1,0:T(8,128)(2,1)S(1)} custom-call(bf16[4,16,2,4,16,256]{5,4,3,2,1,0:T(8,128)(2,1)} %copy-done.1, bf16[16,16,128]{2,1,0:T(8,128)(2,1)S(1)} %get-tuple-element.9.extra, f32[8,128]{1,0:T(8,128)S(1)} %get-tuple-element.10.coef), custom_call_target="tpu_custom_call" | custom-call | tf_op jit(solution)/shard_map/exchange/pallas_call | solution.py:496
  100.1 0.0 copy-done.2
  100.1 0.0 copy-done.5
  100.1 0.0 copy-done.6
  100.1 4.8 %analysis.1 = bf16[8,128,256]{2,1,0:T(8,128)(2,1)} custom-call(bf16[8,128,256]{2,1,0:T(8,128)(2,1)S(1)} %copy-done.2, s32[2,8,128]{2,1,0:T(8,128)S(1)} %copy-done.5, f32[2,8,128]{2,1,0:T(8,128)S(1)} %copy-done.6, bf16[24,256,256]{2,1,0:T(8,128)(2,1)S(1)} %exchange.1.window), custom_call_target="tpu_custom_call" | custom-call | tf_op jit(solution)/shard_map/analysis/pallas_call | solution.py:565
Async XLA Ops:
  2.3 3.4 %copy-start = (bf16[32,512,256]{2,1,0:T(8,128)(2,1)S(1)}, bf16[32,512,256]{2,1,0:T(8,128)(2,1)}, u32[]{:S(2)}) copy-start(bf16[32,512,256]{2,1,0:T(8,128)(2,1)} %pert_hbm.1) | copy-start | bytes 25165828
  5.7 0.8 copy-start.3
  6.4 0.8 copy-start.4
  7.2 0.7 copy-start.7
  7.8 0.7 copy-start.8
  34.1 1.9 %copy-start.1 = (bf16[4,16,2,4,16,256]{5,4,3,2,1,0:T(8,128)(2,1)}, bf16[4,16,2,4,16,256]{5,4,3,2,1,0:T(8,128)(2,1)S(1)}, u32[]{:S(2)}) copy-start(bf16[4,16,2,4,16,256]{5,4,3,2,1,0:T(8,128)(2,1)S(1)} %get-tuple-element.8.packed) | copy-start | bytes 12582916
  36.0 64.1 %copy-start.2 = (bf16[8,128,256]{2,1,0:T(8,128)(2,1)S(1)}, bf16[8,128,256]{2,1,0:T(8,128)(2,1)}, u32[]{:S(2)}) copy-start(bf16[8,128,256]{2,1,0:T(8,128)(2,1)} %background.1) | copy-start | bytes 1572868
  36.0 64.1 %copy-start.5 = (s32[2,8,128]{2,1,0:T(8,128)S(1)}, s32[2,8,128]{2,1,0:T(8,128)}, u32[]{:S(2)}) copy-start(s32[2,8,128]{2,1,0:T(8,128)} %stencil.1) | copy-start | bytes 24580
  36.0 64.1 %copy-start.6 = (f32[2,8,128]{2,1,0:T(8,128)S(1)}, f32[2,8,128]{2,1,0:T(8,128)}, u32[]{:S(2)}) copy-start(f32[2,8,128]{2,1,0:T(8,128)} %frac.1) | copy-start | bytes 24580
where the time goes:
time: 106 us; the launch traced here: 105 us
  Pallas kernels  94.4 us (89%)
  local copies, waits for them, and re-layouts  10.4 us (10%)
    pallas_call x1, Pallas kernels, exchange(): pl.pallas_call(exchange_kernel, out_shape=jax.ShapeDtypeStruct((24, 256,...  64.1 us
    pallas_call x1, Pallas kernels, moments(): pl.pallas_call(moments_kernel, out_shape=(jax.ShapeDtypeStruct((4, 16, 2,...  25.6 us
    unnamed x21, local copies, waits for them, and re-layouts  10.4 us
    pallas_call x1, Pallas kernels, analyse(): pl.pallas_call(analysis_kernel, out_shape=jax.ShapeDtypeStruct((8, HALF,...  4.78 us

commit v1 on v0

v1 whole, which is shorter than its diff:
```python
import jax
import jax.numpy as jnp
from jax import lax
from jax.experimental import pallas as pl
from jax.experimental.pallas import tpu as pltpu
from jax.sharding import PartitionSpec as P

MEMBERS = 256
NOBS = 512
BAT = 32
TOP = 3
PTS = 8
ITERS = 6
HALF = 128
MESH = pl.DeviceIdType.MESH
F32 = jnp.float32
BF16 = jnp.bfloat16
COPIES = 64
GROUP = 4
CENTRE = MEMBERS - 1


def iota(shape, dim):
    return lax.broadcasted_iota(jnp.int32, shape, dim)


def dot(a, b):
    return jnp.dot(a, b, preferred_element_type=F32)


def dot_last(a, b):
    return lax.dot_general(a, b, (((1,), (1,)), ((), ())), preferred_element_type=F32)


def flip(x, z, dim):
    if dim == 0:
        return x + 1 - 2 * (x % 2), z
    if dim == 1:
        return 3 - x, z
    if dim == 2:
        return x, z + 1 - 2 * (z % 2)
    return x, 3 - z


def gray_bits(x, z):
    high_x, high_z = x // 2, z // 2
    low_x, low_z = (x % 2 + high_x) % 2, (z % 2 + high_z) % 2
    return (low_x, high_x, low_z, high_z)


def root_iteration(e_s, eb_s, z_s, scal, k):
    new = []
    for p in range(4):
        m, z = scal[p]
        f = 1.5 - 0.5 * m
        e = e_s[p]
        eb = eb_s[p]
        if k == 0:
            z_s[p] = -0.5 * e
        else:
            r = z_s[p]
            z_s[p] = f * r - 0.5 * (dot(r.astype(BF16), eb) + z * e)
        if k < ITERS - 1:
            g = m * f
            h = (f - 0.5 * m) * e - 0.5 * dot(eb, eb)
            e_new = f * h - 0.5 * (g * e + dot(h.astype(BF16), eb))
            e_s[p] = e_new
            eb_s[p] = e_new.astype(BF16)
        new.append((m * f * f, z * f))
    return new


def step_kernel(
    owner_h,
    points_h,
    count_h,
    len_h,
    weight_h,
    innov_h,
    taper_h,
    pert_h,
    back_h,
    stencil_h,
    frac_h,
    out_ref,
    pert,
    weight,
    innov,
    taper,
    owner_v,
    points_v,
    count_v,
    len_s,
    back,
    stencil,
    frac,
    wide_w,
    wide_i,
    source_v,
    source_s,
    coef,
    held,
    coef_n,
    coef_d,
    send3,
    recv3,
    send4,
    recv4,
    mine1,
    total,
    xheld,
    xsend3,
    xrecv3,
    xsend4,
    xrecv4,
    xmine1,
    xtotal,
    e_s,
    eb_s,
    z_s,
    window,
    lhs_s,
    xlhs_s,
    cells,
    mean_s,
    mixed,
    small_sems,
    pert_sems,
    first_send,
    first_recv,
    send_sems,
    recv_sems,
):
    lat, lon = lax.axis_index("lat"), lax.axis_index("lon")
    x, z = lon // 4, lon % 4
    odd = lat % 2
    lead = (odd, 1 - odd)

    def to(dim):
        hx, hz = flip(x, z, dim % 4)
        return (lat, hx * 4 + hz)

    east, west = (lat, (lon + 1) % 16), (lat, (lon + 15) % 16)
    outer, inner = ((lat + 7 + 2 * odd) % 8, lon), (lat + 1 - 2 * odd, lon)

    barrier = pltpu.get_barrier_semaphore()
    peers = [to(d) for d in range(4)] + [east, west, outer, inner]
    for peer in peers:
        pl.semaphore_signal(barrier, inc=1, device_id=peer, device_id_type=MESH)

    small = []
    for n, (src, dst) in enumerate(
        (
            (owner_h, owner_v),
            (points_h, points_v),
            (count_h, count_v),
            (taper_h, taper),
            (len_h, len_s),
            (weight_h, weight),
            (innov_h, innov),
            (stencil_h, stencil),
            (frac_h, frac),
            (back_h, back),
        )
    ):
        small.append(pltpu.make_async_copy(src, dst, small_sems.at[n]))
    for c in small[:7]:
        c.start()
    fetches = []
    for g in range(BAT // GROUP):
        rows = pl.ds(g * GROUP, GROUP)
        fetches.append(pltpu.make_async_copy(pert_h.at[rows], pert.at[rows], pert_sems.at[g]))
        fetches[g].start()
    for c in small[7:]:
        c.start()

    for c in small[:4]:
        c.wait()
    owner_row = owner_v[...]
    turned = jnp.broadcast_to(owner_row, (BAT, BAT)).T
    before = (turned == owner_row) & (iota((BAT, BAT), 0) < iota((BAT, BAT), 1))
    rank_row = jnp.sum(jnp.where(before, 1, 0), axis=0, keepdims=True)
    mine = gray_bits(x, z)
    theirs = gray_bits(owner_row // 4, owner_row % 4)
    rel_row = jnp.zeros((1, BAT), jnp.int32)
    for d in range(4):
        rel_row = rel_row + ((theirs[d] + mine[d]) % 2) * (1 << d)
    slots = iota((HALF, BAT), 0)
    slot_rows = jnp.broadcast_to(rel_row * 4 + rank_row, (BAT, BAT)).T
    fills = jnp.broadcast_to(slot_rows[:, 0:1], (BAT, HALF)) == iota((BAT, HALF), 1)
    source = jnp.sum(jnp.where(fills, iota((BAT, HALF), 0), 0), axis=0, keepdims=True)
    source_v[...] = jnp.broadcast_to(source, (PTS, HALF))
    table = pltpu.make_async_copy(source_v, source_s, small_sems.at[10])
    table.start()
    points, listed = points_v[...], taper[...].astype(F32)
    q = iota((PTS, BAT), 0)
    point = jnp.where(
        q < 4, (q // 2) * 4 + (q % 2) * 3, ((q - 4) // 2) * 4 + 1 + q % 2
    )
    weights = jnp.zeros((PTS, BAT), F32)
    for j in range(TOP):
        hit = (point == points[j : j + 1, :]) & (count_v[...] > j)
        weights = weights + jnp.where(hit, listed[j : j + 1, :], 0.0)
    spot = jnp.where(slots == owner_row * 4 + rank_row, 1.0, 0.0).astype(BF16)
    coef[...] = dot_last(weights.astype(BF16), spot)
    for c in small[4:7]:
        c.wait()
    wide_w[...] = weight[...].astype(F32)
    wide_i[...] = innov[...].astype(F32)
    table.wait()
    pl.semaphore_wait(barrier, len(peers))

    used = []

    def push(src, dst, peer):
        n = len(used)
        c = pltpu.make_async_remote_copy(
            src_ref=src,
            dst_ref=dst,
            send_sem=send_sems.at[n],
            recv_sem=recv_sems.at[n],
            device_id=peer,
            device_id_type=MESH,
        )
        c.start()
        used.append(c)
        return c

    def first_copy(k, at):
        return pltpu.make_async_remote_copy(
            src_ref=held.at[k, at + 8, :, 0],
            dst_ref=held.at[k, at, :, 1],
            send_sem=first_send.at[k, at],
            recv_sem=first_recv.at[k, at],
            device_id=to(k),
            device_id_type=MESH,
        )

    row, col = iota((HALF, HALF), 0), iota((HALF, HALF), 1)
    tail_row = iota((16, NOBS), 0)
    for c in fetches:
        c.wait()

    def one_owner(n, carry):
        rel = 15 - n
        bits = [(rel // (1 << d)) % 2 for d in range(4)]
        place = [
            bits[k] * 8 + bits[(k + 1) % 4] * 4 + bits[(k + 2) % 4] * 2 + bits[(k + 3) % 4]
            for k in range(4)
        ]
        kinds = []
        for s in range(4):
            b = jnp.minimum(jnp.maximum(source_s[0, rel * 4 + s], 0), BAT - 1)
            p = pert[b]
            live = iota((1, NOBS), 1) < len_s[0, b]
            w = jnp.where(live, wide_w[pl.ds(b, 1), :], 0.0)
            wi = w * wide_i[pl.ds(b, 1), :]
            high = wi.astype(BF16).astype(F32)
            tail = jnp.where(tail_row == 0, high, jnp.where(tail_row == 1, wi - high, 0.0))
            scaled = p.T * w.astype(BF16)
            acc = dot(jnp.concatenate([scaled, tail.astype(BF16)], axis=0), p)
            corner = acc[HALF:256, HALF:256]
            left = jnp.where(col >= row, acc[0:HALF, 0:HALF], corner)
            top = jnp.concatenate([left, acc[0:HALF, HALF:256]], axis=1).astype(BF16)
            for k in range(4):
                for rc in range(2):
                    at = 32 * k + 16 * rc
                    held[k, place[k], rc, 0, s] = top[at : at + 16, :]
            proj = acc[256:257, :] + acc[257:258, :]
            diagonal = jnp.sum(jnp.where(col == row, corner, 0.0), axis=0, keepdims=True)
            kinds += [diagonal, proj[:, 0:HALF], proj[:, HALF:256], jnp.zeros((1, HALF), F32)]
        xheld[place[0], 0] = jnp.concatenate(kinds, axis=0).astype(BF16)
        for k in range(4):

            @pl.when(bits[k] == 1)
            def _():
                first_copy(k, place[k] % 8).start()

        return carry

    cn = [push(coef, coef_n.at[k], to(k)) for k in range(4)]
    lax.fori_loop(0, 16, one_owner, 0)
    x1 = push(xheld.at[8:16, 0], xheld.at[0:8, 1], to(0))
    for k in range(4):
        cn[k].wait_recv()
    cd = [push(coef_n.at[k], coef_d.at[k], to(k + 1)) for k in range(4)]

    def sources(k):
        rows = [coef[...], coef_n[k], coef_n[(k + 1) % 4], coef_d[k]]
        return jnp.concatenate(rows, axis=0).astype(BF16)

    def served(k, pos):
        sx, sz = x, z
        if pos & 2:
            sx, sz = flip(sx, sz, (k + 2) % 4)
        if pos & 1:
            sx, sz = flip(sx, sz, (k + 3) % 4)
        return sx * 4 + sz

    def spread(k, pos, width, each):
        lane = iota((HALF, width), 1)
        pick = jnp.where(
            iota((HALF, width), 0) == served(k, pos) * 4 + (lane // each) % 4, 1.0, 0.0
        ).astype(BF16)
        every = dot(sources(k), pick)
        lane8 = iota((8, width), 1) // (4 * each)
        out = jnp.zeros((8, width), F32)
        for j in range(4):
            out = out + jnp.where(lane8 == j, every[8 * j : 8 * j + 8, :], 0.0)
        return out

    def expand(weights, rows, each):
        width = weights.shape[1]
        keep = iota((rows, width), 1) % each == iota((rows, width), 0)
        blocks = [
            jnp.where(keep, jnp.broadcast_to(weights[p : p + 1, :], (rows, width)), 0.0)
            for p in range(PTS)
        ]
        return jnp.concatenate(blocks, axis=0).astype(BF16)

    def merged(k, pos):
        lhs = lhs_s[k, pos]
        return [
            dot(lhs, held[k, pos, rc].reshape(256, 256)).reshape(PTS, 16, 256) for rc in range(2)
        ]

    def xmerged(pos):
        return dot(xlhs_s[pos][:, 0:64], xheld[pos].reshape(64, HALF))

    for k in range(4):
        cd[k].wait_recv()
    for pos in range(4):
        for k in range(4):
            lhs_s[k, pos] = expand(spread(k, pos, 256, 16), 16, 16)
        xlhs_s[pos] = expand(spread(0, pos, HALF, 4), 8, 4)

    s2a, s2b = [], []
    for k in range(4):
        for at in range(4, 8):
            first_copy(k, at).wait_recv()
        s2a.append(push(held.at[k, 6:8, :, 0:2], held.at[k, 2:4, :, 2:4], to(k + 1)))
    for k in range(4):
        s2b.append(push(held.at[k, 4:6, :, 0:2], held.at[k, 0:2, :, 2:4], to(k + 1)))
    x1.wait_recv()
    x2 = push(xheld.at[4:8, 0:2], xheld.at[0:4, 2:4], to(1))

    for c in small[7:]:
        c.wait()
    corner_id = (stencil[0] - (lat * 2 - 1)) * 6 + (stencil[1] - lon * 4 + 65) % 64
    fy, fx = frac[0], frac[1]
    corners = (
        (0, (1.0 - fy) * (1.0 - fx)),
        (6, fy * (1.0 - fx)),
        (1, (1.0 - fy) * fx),
        (7, fy * fx),
    )
    for t in range(4):
        turned = back[2 * t : 2 * t + 2].reshape(256, 256).T.astype(F32)
        mean = jnp.sum(turned, axis=0, keepdims=True) * (1.0 / MEMBERS)
        mean_s[t] = jnp.broadcast_to(mean, (8, 256))
        deviation = (turned - mean).astype(BF16).astype(F32)
        for j in range(24):
            value = jnp.zeros((8, HALF), F32)
            for add, share in corners:
                value = value + jnp.where(corner_id + add == j, share, 0.0)
            share = jnp.concatenate([value[2 * t : 2 * t + 1], value[2 * t + 1 : 2 * t + 2]], axis=1)
            cells[j, t] = (deviation * share).astype(BF16)

    for k in range(4):
        for at in range(4):
            first_copy(k, at).wait_recv()
    s3a, s3b = [], []
    for pos in (3, 2):
        for k in range(4):
            if pos == 3:
                s2a[k].wait_recv()
            for rc, value in enumerate(merged(k, pos)):
                send3[k, pos - 2, :, 16 * rc : 16 * rc + 16, :] = value.astype(BF16)
            if pos == 3:
                s3a.append(push(send3.at[k, 1], recv3.at[k, 1], to(k + 2)))
            else:
                for h in range(2):
                    span = pl.ds(4 * h, 4)
                    s3b.append(push(send3.at[k, 0, span], recv3.at[k, 0, span], to(k + 2)))
    x2.wait_recv()
    for pos in (3, 2):
        xsend3[pos - 2] = xmerged(pos).astype(BF16)
    x3 = push(xsend3, xrecv3, to(2))

    for pos in (1, 0):
        for k in range(4):
            if pos == 1:
                s2b[k].wait_recv()
            for rc, value in enumerate(merged(k, pos)):
                if pos == 1:
                    mine1[k, :, 16 * rc : 16 * rc + 16, :] = value
                else:
                    at = 32 * k + 16 * rc
                    total[:, at : at + 16, :] = value
    xmine1[...] = xmerged(1)
    xtotal[...] = xmerged(0)

    s4 = []

    def half4(k, h):
        span = pl.ds(4 * h, 4)
        return push(send4.at[k, span], recv4.at[k, span], to(k + 3))

    for k in range(4):
        s3a[k].wait_recv()
        send4[k] = (mine1[k] + recv3[k, 1].astype(F32)).astype(BF16)
        s4.append(half4(k, 0))
    x3.wait_recv()
    xsend4[...] = (xmine1[...] + xrecv3[1].astype(F32)).astype(BF16)
    x4 = push(xsend4, xrecv4, to(3))
    for k in range(4):
        s4.append(half4(k, 1))
    x4.wait_recv()
    xtotal[...] += xrecv3[0].astype(F32) + xrecv4[...].astype(F32)

    outside, inside, side = [], [], []

    def rim(a, slot, column):
        if a == 0:
            outside.append((column, push(window.at[slot], window.at[18 * (1 - odd) + column], outer)))
        else:
            inside.append((column, push(window.at[slot], window.at[18 * odd + column], inner)))

    def corners_on():
        for a in range(2):
            for j in range(2):
                side[2 * a + j].wait_recv()
                column = 5 - 5 * j
                rim(a, (lead[a] + 1) * 6 + column, column)

    eye = jnp.where(row == col, float(CENTRE), 0.0)
    for g in range(2):
        scal, scales = [], []
        for k in range(4):
            s3b[2 * k + g].wait_recv()
            s4[4 * g + k].wait_recv()
        for i in range(4):
            p = 4 * g + i
            for k in range(4):
                total[p, 32 * k : 32 * k + 32, :] += recv3[k, 0, p].astype(F32) + recv4[
                    k, p
                ].astype(F32)
            left, right = total[p, :, 0:HALF], total[p, :, HALF:256]
            turned = left.T
            a = jnp.where(col >= row, left, turned) + eye
            c = jnp.where(col < row, left, turned)
            c = jnp.where(col == row, xtotal[8 * p : 8 * p + 1, :], c) + eye
            square = jnp.sum(a * a + c * c + 2.0 * (right * right), keepdims=True)
            trace = jnp.sum(jnp.where(row == col, a + c, 0.0), keepdims=True)
            scale = jnp.sqrt(square)
            inverse = 1.0 / scale
            mean = trace * (1.0 / MEMBERS)
            off = jnp.where(row == col, mean, 0.0)
            a, c, b = (a - off) * inverse, (c - off) * inverse, right * inverse
            e_s[i] = jnp.concatenate(
                [jnp.concatenate([a, b], axis=1), jnp.concatenate([b.T, c], axis=1)], axis=0
            )
            eb_s[i] = e_s[i].astype(BF16)
            scal.append((mean * inverse, jnp.ones((1, 1), F32)))
            scales.append(scale)
        for k in range(ITERS):
            scal = root_iteration(e_s, eb_s, z_s, scal, k)
            if g == 1 and k == 3:
                corners_on()
        big = iota((256, 256), 0) == iota((256, 256), 1)
        tail16 = iota((16, 256), 0)
        for a in range(2):
            for j in range(2):
                i = 2 * lead[a] + j
                flag = jnp.full((1, 1), lead[a], jnp.int32) == 1
                zd = jnp.where(flag, scal[2 + j][1], scal[j][1])
                scale = jnp.where(flag, scales[2 + j], scales[j])
                r = z_s[i]
                high = r.astype(BF16)
                low = (r - high.astype(F32)).astype(BF16)

                def apply(v):
                    vh = v.astype(BF16).astype(F32)
                    both = jnp.where(tail16 == 0, vh, jnp.where(tail16 == 1, v - vh, 0.0)).astype(
                        BF16
                    )
                    w = dot(both, high) + dot(both, low)
                    return zd * v + w[0:1, :] + w[1:2, :]

                kinds = xtotal[pl.ds(pl.multiple_of(8 * (4 * g + i), 8), 8), :]
                shift = jnp.concatenate([kinds[1:2], kinds[2:3]], axis=1)
                mw = apply(apply(shift)) / scale
                amp = jnp.sqrt(float(CENTRE) / scale)
                full = amp * (r + jnp.where(big, zd, 0.0)) + mw
                column = 1 + 3 * j if g == 0 else 2 + j
                slot = (lead[a] + 1) * 6 + column
                window[slot] = full.astype(BF16)
                if g == 0:
                    across = window.at[(lead[a] + 1) * 6 + 5 - 5 * j]
                    side.append(push(window.at[slot], across, west if j == 0 else east))
                rim(a, slot, column)

    def gather(slots, start=False):
        for t in range(4):
            part = dot(window[slots[0]], cells[slots[0], t])
            for n in slots[1:]:
                part = part + dot(window[n], cells[n, t])
            mixed[t] = part if start else mixed[t] + part

    gather([6 * r + c for r in (1, 2) for c in range(6)], start=True)
    for column, c in inside:
        c.wait_recv()
    gather([18 * (1 - odd) + column for column in range(6)])
    for column, c in outside:
        if column not in (2, 3):
            c.wait_recv()
    gather([18 * odd + column for column in (0, 1, 4, 5)])
    for column, c in outside:
        if column in (2, 3):
            c.wait_recv()
    for t in range(4):
        far = 18 * odd
        part = mixed[t] + dot(window[far + 2], cells[far + 2, t]) + dot(
            window[far + 3], cells[far + 3, t]
        )
        whole = (part + mean_s[t][0:1, :]).astype(BF16)
        out_ref[2 * t : 2 * t + 2] = whole.T.reshape(2, HALF, 256)
    for k in range(4):
        for at in range(8):
            first_copy(k, at).wait_send()
    for c in used:
        c.wait_send()


def step(args):
    hbm = pl.BlockSpec(memory_space=pl.ANY)
    i32 = jnp.int32
    vm = pltpu.VMEM
    return pl.pallas_call(
        step_kernel,
        out_shape=jax.ShapeDtypeStruct((8, HALF, 256), BF16),
        in_specs=[hbm] * len(args),
        out_specs=pl.BlockSpec(memory_space=pltpu.VMEM),
        scratch_shapes=[
            vm((BAT, NOBS, MEMBERS), BF16),
            vm((BAT, NOBS), BF16),
            vm((BAT, NOBS), BF16),
            vm((TOP, BAT), BF16),
            vm((1, BAT), i32),
            vm((TOP, BAT), i32),
            vm((1, BAT), i32),
            pltpu.SMEM((1, BAT), i32),
            vm((8, HALF, 256), BF16),
            vm((2, 8, HALF), i32),
            vm((2, 8, HALF), F32),
            vm((BAT, NOBS), F32),
            vm((BAT, NOBS), F32),
            vm((PTS, HALF), i32),
            pltpu.SMEM((PTS, HALF), i32),
            vm((PTS, HALF), F32),
            vm((4, 16, 2, 4, 4, 16, 256), BF16),
            vm((4, PTS, HALF), F32),
            vm((4, PTS, HALF), F32),
            vm((4, 2, PTS, 32, 256), BF16),
            vm((4, 2, PTS, 32, 256), BF16),
            vm((4, PTS, 32, 256), BF16),
            vm((4, PTS, 32, 256), BF16),
            vm((4, PTS, 32, 256), F32),
            vm((PTS, HALF, 256), F32),
            vm((16, 4, 16, HALF), BF16),
            vm((2, 64, HALF), BF16),
            vm((2, 64, HALF), BF16),
            vm((64, HALF), BF16),
            vm((64, HALF), BF16),
            vm((64, HALF), F32),
            vm((64, HALF), F32),
            vm((4, 256, 256), F32),
            vm((4, 256, 256), BF16),
            vm((4, 256, 256), F32),
            vm((24, 256, 256), BF16),
            vm((4, 4, HALF, 256), BF16),
            vm((4, 64, HALF), BF16),
            vm((24, 4, 256, 256), BF16),
            vm((4, 8, 256), F32),
            vm((4, 256, 256), F32),
            pltpu.SemaphoreType.DMA((11,)),
            pltpu.SemaphoreType.DMA((BAT // GROUP,)),
            pltpu.SemaphoreType.DMA((4, 8)),
            pltpu.SemaphoreType.DMA((4, 8)),
            pltpu.SemaphoreType.DMA((COPIES,)),
            pltpu.SemaphoreType.DMA((COPIES,)),
        ],
        compiler_params=pltpu.CompilerParams(
            collective_id=0, has_side_effects=True, vmem_limit_bytes=67043328
        ),
        name="step",
    )(*args)


def on_device(
    obs_pert,
    obs_weight,
    innovation,
    batch_len,
    batch_owner,
    batch_points,
    batch_count,
    batch_taper,
    background,
    stencil,
    frac,
):
    return step(
        (
            batch_owner.T,
            batch_points.T,
            batch_count.reshape(1, BAT),
            batch_len,
            obs_weight,
            innovation,
            batch_taper.T,
            obs_pert,
            background,
            stencil,
            frac,
        )
    )


def solution(mesh):
    return jax.shard_map(
        on_device,
        mesh=mesh,
        in_specs=(
            P(("lat", "lon"), None, None),
            P(("lat", "lon"), None),
            P(("lat", "lon"), None),
            P(("lat", "lon"), None),
            P(("lat", "lon"), None),
            P(("lat", "lon"), None),
            P(("lat", "lon")),
            P(("lat", "lon"), None),
            P("lat", "lon", None),
            P(None, "lat", "lon"),
            P(None, "lat", "lon"),
        ),
        out_specs=P("lat", "lon", None),
        check_vma=False,
    )
```

time: 106 us -> 69.3 us (0.65)
  Pallas kernels: 94.4 us -> 67.3 us
  local copies, waits for them, and re-layouts: 10.4 us -> 1.87 us
    pallas_call x3 -> x1, Pallas kernels: 94.4 us -> 67.3 us  [step(): pl.pallas_call(step_kernel, out_shape=jax.ShapeDtypeStruct((8, HALF, 256)...]
    unnamed x21 -> x1, local copies, waits for them, and re-layouts: 10.4 us -> 1.87 us
where the time goes in v1:
time: 69.3 us; the launch traced here: 69.2 us
  Pallas kernels  67.3 us (97%)
  local copies, waits for them, and re-layouts  1.87 us (3%)
    pallas_call x1, Pallas kernels, step(): pl.pallas_call(step_kernel, out_shape=jax.ShapeDtypeStruct((8, HALF, 256)...  67.3 us
    unnamed x1, local copies, waits for them, and re-layouts  1.87 us

profile of v1, /device:TPU:1, one launch (start us, length us, event | category | flops | bytes accessed | tf_op | source)
XLA Modules:
  0.0 69.2 jit_solution(9631830418020083434)
XLA Ops:
  0.0 67.3 %step.1 = bf16[8,128,256]{2,1,0:T(8,128)(2,1)} custom-call(s32[1,32]{1,0:T(1,128)} %bitcast.6, s32[3,32]{1,0:T(4,128)} %bitcast.4, s32[1,32]{1,0:T(1,128)} %bitcast.7, s32[1,32]{1,0:T(1,128)} %len_h.1, bf16[32,512]{1,0:T(8,128)(2,1)} %weight_h.1, bf16[32,512]{1,0:T(8,128)(2,1)} %innov_h.1, bf16[3,32]{1,0:T(4,128)(2,1)} %bitcast.5, ...), custom_call_target="tpu_custom_call" | custom-call | tf_op jit(solution)/shard_map/step/pallas_call | solution.py:539
  67.3 1.9 %copy.13 = bf16[8,128,256]{2,1,0:T(8,128)(2,1)} copy(bf16[8,128,256]{2,1,0:T(8,128)(2,1)} %step.1) | data formatting | bytes 1048576

commit v2 on v1

--- a/solution.py
+++ b/solution.py
@@ -48,26 +48,27 @@
     return (low_x, high_x, low_z, high_z)
 
 
-def root_iteration(e_s, eb_s, z_s, scal, k):
-    new = []
-    for p in range(4):
-        m, z = scal[p]
-        f = 1.5 - 0.5 * m
-        e = e_s[p]
-        eb = eb_s[p]
-        if k == 0:
-            z_s[p] = -0.5 * e
-        else:
-            r = z_s[p]
-            z_s[p] = f * r - 0.5 * (dot(r.astype(BF16), eb) + z * e)
-        if k < ITERS - 1:
-            g = m * f
-            h = (f - 0.5 * m) * e - 0.5 * dot(eb, eb)
-            e_new = f * h - 0.5 * (g * e + dot(h.astype(BF16), eb))
-            e_s[p] = e_new
-            eb_s[p] = e_new.astype(BF16)
-        new.append((m * f * f, z * f))
-    return new
+def root_iteration(phi_s, low_s, xi_s, scal, k):
+    four, last = range(4), k == ITERS - 1
+    f = [1.5 - 0.5 * scal[p][0] for p in four]
+    m_new = [scal[p][0] * f[p] * f[p] for p in four]
+    back = [-0.5 * scal[p][0] / f[p] for p in four]
+    if not last:
+        square = [dot(low_s[p], low_s[p]) for p in four]
+    if k:
+        grown = [dot(xi_s[p].astype(BF16), low_s[p]) for p in four]
+    if not last:
+        both = [((2.0 + back[p]) * phi_s[p] + square[p]).astype(BF16) for p in four]
+        cubic = [dot(both[p], low_s[p]) for p in four]
+    for p in four:
+        xi_s[p] = (xi_s[p] + phi_s[p]) + grown[p] if k else phi_s[p]
+    if not last:
+        for p in four:
+            ratio = f[p] * f[p] * f[p] / (1.5 - 0.5 * m_new[p])
+            phi_new = (ratio * (1.0 + 2.0 * back[p])) * phi_s[p] + ratio * cubic[p]
+            phi_s[p] = phi_new
+            low_s[p] = phi_new.astype(BF16)
+    return [(m_new[p], scal[p][1] * f[p]) for p in four]
 
 
 def step_kernel(
@@ -119,11 +120,13 @@
     eb_s,
     z_s,
     window,
+    rims,
     lhs_s,
     xlhs_s,
     cells,
     mean_s,
     mixed,
+    done,
     small_sems,
     pert_sems,
     first_send,
@@ -318,12 +321,6 @@
         ]
         return jnp.concatenate(blocks, axis=0).astype(BF16)
 
-    def merged(k, pos):
-        lhs = lhs_s[k, pos]
-        return [
-            dot(lhs, held[k, pos, rc].reshape(256, 256)).reshape(PTS, 16, 256) for rc in range(2)
-        ]
-
     def xmerged(pos):
         return dot(xlhs_s[pos][:, 0:64], xheld[pos].reshape(64, HALF))
 
@@ -369,52 +366,63 @@
     for k in range(4):
         for at in range(4):
             first_copy(k, at).wait_recv()
-    s3a, s3b = [], []
-    for pos in (3, 2):
+
+    def merge(k, pos, g):
+        lhs = lhs_s[k, pos, 64 * g : 64 * g + 64, :]
+        return [dot(lhs, held[k, pos, rc].reshape(256, 256)).reshape(4, 16, 256) for rc in range(2)]
+
+    def send_on(pos, g):
         for k in range(4):
-            if pos == 3:
+            if (pos, g) == (3, 0):
                 s2a[k].wait_recv()
-            for rc, value in enumerate(merged(k, pos)):
-                send3[k, pos - 2, :, 16 * rc : 16 * rc + 16, :] = value.astype(BF16)
-            if pos == 3:
-                s3a.append(push(send3.at[k, 1], recv3.at[k, 1], to(k + 2)))
-            else:
-                for h in range(2):
-                    span = pl.ds(4 * h, 4)
-                    s3b.append(push(send3.at[k, 0, span], recv3.at[k, 0, span], to(k + 2)))
+            span = slice(4 * g, 4 * g + 4)
+            for rc, value in enumerate(merge(k, pos, g)):
+                send3[k, pos - 2, span, 16 * rc : 16 * rc + 16, :] = value.astype(BF16)
+            s3[pos, g, k] = push(send3.at[k, pos - 2, span], recv3.at[k, pos - 2, span], to(k + 2))
+
+    def keep_own(g):
+        for k in range(4):
+            if g == 0:
+                s2b[k].wait_recv()
+            span = slice(4 * g, 4 * g + 4)
+            for rc, value in enumerate(merge(k, 1, g)):
+                mine1[k, span, 16 * rc : 16 * rc + 16, :] = value
+            for rc, value in enumerate(merge(k, 0, g)):
+                at = 32 * k + 16 * rc
+                total[span, at : at + 16, :] = value
+
+    def last_step(g):
+        for k in range(4):
+            s3[3, g, k].wait_recv()
+            span = slice(4 * g, 4 * g + 4)
+            send4[k, span] = (mine1[k, span] + recv3[k, 1, span].astype(F32)).astype(BF16)
+            s4[g, k] = push(send4.at[k, span], recv4.at[k, span], to(k + 3))
+
+    s3, s4 = {}, {}
+    send_on(3, 0)
+    send_on(2, 0)
     x2.wait_recv()
     for pos in (3, 2):
         xsend3[pos - 2] = xmerged(pos).astype(BF16)
     x3 = push(xsend3, xrecv3, to(2))
-
-    for pos in (1, 0):
-        for k in range(4):
-            if pos == 1:
-                s2b[k].wait_recv()
-            for rc, value in enumerate(merged(k, pos)):
-                if pos == 1:
-                    mine1[k, :, 16 * rc : 16 * rc + 16, :] = value
-                else:
-                    at = 32 * k + 16 * rc
-                    total[:, at : at + 16, :] = value
+    send_on(3, 1)
+    keep_own(0)
     xmine1[...] = xmerged(1)
     xtotal[...] = xmerged(0)
-
-    s4 = []
-
-    def half4(k, h):
-        span = pl.ds(4 * h, 4)
-        return push(send4.at[k, span], recv4.at[k, span], to(k + 3))
-
-    for k in range(4):
-        s3a[k].wait_recv()
-        send4[k] = (mine1[k] + recv3[k, 1].astype(F32)).astype(BF16)
-        s4.append(half4(k, 0))
+    last_step(0)
     x3.wait_recv()
     xsend4[...] = (xmine1[...] + xrecv3[1].astype(F32)).astype(BF16)
     x4 = push(xsend4, xrecv4, to(3))
+    send_on(2, 1)
+    keep_own(1)
     for k in range(4):
-        s4.append(half4(k, 1))
+        for at in range(8):
+            first_copy(k, at).wait_send()
+    early = 18
+    for c in used[:early]:
+        c.wait_send()
+    last_step(1)
+    late = len(used)
     x4.wait_recv()
     xtotal[...] += xrecv3[0].astype(F32) + xrecv4[...].astype(F32)
 
@@ -422,23 +430,43 @@
 
     def rim(a, slot, column):
         if a == 0:
-            outside.append((column, push(window.at[slot], window.at[18 * (1 - odd) + column], outer)))
+            outside.append((column, push(rims.at[slot], rims.at[18 * (1 - odd) + column], outer)))
         else:
-            inside.append((column, push(window.at[slot], window.at[18 * odd + column], inner)))
-
-    def corners_on():
-        for a in range(2):
-            for j in range(2):
-                side[2 * a + j].wait_recv()
-                column = 5 - 5 * j
-                rim(a, (lead[a] + 1) * 6 + column, column)
+            inside.append((column, push(rims.at[slot], rims.at[18 * odd + column], inner)))
+
+    def unfold(n):
+        fold = rims[n, 0:HALF, 0:HALF].astype(F32)
+        right = rims[n, 0:HALF, HALF:256]
+        turned = fold.T
+        a = jnp.where(col >= row, fold, turned)
+        c = jnp.where(col < row, fold, turned)
+        last = rims[n, HALF:144, :]
+        c = jnp.where(col == row, last[:, 0:HALF].astype(F32)[2:3, :], c)
+        window[n, 0:HALF, :] = jnp.concatenate([a.astype(BF16), right], axis=1)
+        window[n, HALF:256, :] = jnp.concatenate([right.T, c.astype(BF16)], axis=1)
+        window[n, 256:272, :] = last
+
+    def corners_on(a):
+        for j in range(2):
+            side[2 * a + j].wait_recv()
+            column = 5 - 5 * j
+            rim(a, (lead[a] + 1) * 6 + column, column)
+        for column in (0, 5):
+            unfold((lead[a] + 1) * 6 + column)
+
+    def gather(slots, start=False):
+        for t in range(4):
+            part = dot(window[slots[0]], cells[slots[0], t])
+            for n in slots[1:]:
+                part = part + dot(window[n], cells[n, t])
+            mixed[t] = part if start else mixed[t] + part
 
     eye = jnp.where(row == col, float(CENTRE), 0.0)
     for g in range(2):
         scal, scales = [], []
         for k in range(4):
-            s3b[2 * k + g].wait_recv()
-            s4[4 * g + k].wait_recv()
+            s3[2, g, k].wait_recv()
+            s4[g, k].wait_recv()
         for i in range(4):
             p = 4 * g + i
             for k in range(4):
@@ -456,7 +484,8 @@
             inverse = 1.0 / scale
             mean = trace * (1.0 / MEMBERS)
             off = jnp.where(row == col, mean, 0.0)
-            a, c, b = (a - off) * inverse, (c - off) * inverse, right * inverse
+            slope = -0.5 * inverse / (1.5 - 0.5 * mean * inverse)
+            a, c, b = (a - off) * slope, (c - off) * slope, right * slope
             e_s[i] = jnp.concatenate(
                 [jnp.concatenate([a, b], axis=1), jnp.concatenate([b.T, c], axis=1)], axis=0
             )
@@ -465,71 +494,92 @@
             scales.append(scale)
         for k in range(ITERS):
             scal = root_iteration(e_s, eb_s, z_s, scal, k)
+            if g == 1 and k in (2, 3):
+                corners_on(k - 2)
             if g == 1 and k == 3:
-                corners_on()
+                for c in used[early:late]:
+                    c.wait_send()
+                gather([6 * r + c for r in (1, 2) for c in (0, 1, 4, 5)], start=True)
         big = iota((256, 256), 0) == iota((256, 256), 1)
         tail16 = iota((16, 256), 0)
+        turns = []
         for a in range(2):
             for j in range(2):
                 i = 2 * lead[a] + j
                 flag = jnp.full((1, 1), lead[a], jnp.int32) == 1
                 zd = jnp.where(flag, scal[2 + j][1], scal[j][1])
                 scale = jnp.where(flag, scales[2 + j], scales[j])
+                kinds = xtotal[pl.ds(pl.multiple_of(8 * (4 * g + i), 8), 8), :]
+                shift = jnp.concatenate([kinds[1:2], kinds[2:3]], axis=1)
+                turns.append([a, j, i, zd, scale, shift])
+        for again in range(2):
+            moved = []
+            for a, j, i, zd, scale, v in turns:
                 r = z_s[i]
                 high = r.astype(BF16)
                 low = (r - high.astype(F32)).astype(BF16)
-
-                def apply(v):
-                    vh = v.astype(BF16).astype(F32)
-                    both = jnp.where(tail16 == 0, vh, jnp.where(tail16 == 1, v - vh, 0.0)).astype(
-                        BF16
-                    )
-                    w = dot(both, high) + dot(both, low)
-                    return zd * v + w[0:1, :] + w[1:2, :]
-
-                kinds = xtotal[pl.ds(pl.multiple_of(8 * (4 * g + i), 8), 8), :]
-                shift = jnp.concatenate([kinds[1:2], kinds[2:3]], axis=1)
-                mw = apply(apply(shift)) / scale
-                amp = jnp.sqrt(float(CENTRE) / scale)
-                full = amp * (r + jnp.where(big, zd, 0.0)) + mw
-                column = 1 + 3 * j if g == 0 else 2 + j
-                slot = (lead[a] + 1) * 6 + column
-                window[slot] = full.astype(BF16)
-                if g == 0:
-                    across = window.at[(lead[a] + 1) * 6 + 5 - 5 * j]
-                    side.append(push(window.at[slot], across, west if j == 0 else east))
-                rim(a, slot, column)
-
-    def gather(slots, start=False):
-        for t in range(4):
-            part = dot(window[slots[0]], cells[slots[0], t])
-            for n in slots[1:]:
-                part = part + dot(window[n], cells[n, t])
-            mixed[t] = part if start else mixed[t] + part
-
-    gather([6 * r + c for r in (1, 2) for c in range(6)], start=True)
+                vh = v.astype(BF16).astype(F32)
+                both = jnp.where(tail16 == 0, vh, jnp.where(tail16 == 1, v - vh, 0.0)).astype(BF16)
+                moved.append(dot(both, high) + dot(both, low))
+            for n, w in enumerate(moved):
+                turns[n][5] = turns[n][3] * (turns[n][5] + w[0:1, :] + w[1:2, :])
+        for a, j, i, zd, scale, v in turns:
+            mw = v / scale
+            amp = jnp.sqrt(float(CENTRE) / scale)
+            whole = (amp * zd) * (z_s[i] + jnp.where(big, 1.0, 0.0))
+            column = 1 + 3 * j if g == 0 else 2 + j
+            slot = (lead[a] + 1) * 6 + column
+            window[slot, 0:256, :] = whole.astype(BF16)
+            corner = whole[HALF:256, HALF:256]
+            fold = jnp.where(col >= row, whole[0:HALF, 0:HALF], corner)
+            rims[slot, 0:HALF, :] = jnp.concatenate([fold, whole[0:HALF, HALF:256]], axis=1).astype(
+                BF16
+            )
+            diagonal = jnp.sum(jnp.where(col == row, corner, 0.0), axis=0, keepdims=True)
+            diagonal = jnp.concatenate([diagonal, jnp.zeros((1, HALF), F32)], axis=1)
+            high = mw.astype(BF16).astype(F32)
+            last = jnp.where(tail16 == 2, diagonal, 0.0)
+            last = jnp.where(tail16 == 0, high, jnp.where(tail16 == 1, mw - high, last)).astype(BF16)
+            rims[slot, HALF:144, :] = last
+            window[slot, 256:272, :] = last
+            if g == 0:
+                across = rims.at[(lead[a] + 1) * 6 + 5 - 5 * j]
+                side.append(push(rims.at[slot], across, west if j == 0 else east))
+            rim(a, slot, column)
+
+    gather([6 * r + c for r in (1, 2) for c in (2, 3)])
     for column, c in inside:
         c.wait_recv()
-    gather([18 * (1 - odd) + column for column in range(6)])
+    near, far = 18 * (1 - odd), 18 * odd
+    for column in range(6):
+        unfold(near + column)
+    gather([near + column for column in range(6)])
     for column, c in outside:
         if column not in (2, 3):
             c.wait_recv()
-    gather([18 * odd + column for column in (0, 1, 4, 5)])
+    for column in (0, 1, 4, 5):
+        unfold(far + column)
+    gather([far + column for column in (0, 1, 4, 5)])
     for column, c in outside:
         if column in (2, 3):
             c.wait_recv()
+    for column in (2, 3):
+        unfold(far + column)
+    outs = []
     for t in range(4):
-        far = 18 * odd
-        part = mixed[t] + dot(window[far + 2], cells[far + 2, t]) + dot(
-            window[far + 3], cells[far + 3, t]
+        part = mixed[t] + (
+            dot(window[far + 2], cells[far + 2, t]) + dot(window[far + 3], cells[far + 3, t])
         )
-        whole = (part + mean_s[t][0:1, :]).astype(BF16)
-        out_ref[2 * t : 2 * t + 2] = whole.T.reshape(2, HALF, 256)
-    for k in range(4):
-        for at in range(8):
-            first_copy(k, at).wait_send()
-    for c in used:
+        shared = part[256:257, :] + part[257:258, :] + mean_s[t][0:1, :]
+        whole = (part[0:256, :] + shared).astype(BF16)
+        done[2 * t : 2 * t + 2] = whole.T.reshape(2, HALF, 256)
+        span = pl.ds(2 * t, 2)
+        outs.append(pltpu.make_async_copy(done.at[span], out_ref.at[span], small_sems.at[t]))
+        outs[t].start()
+    for c in used[late:]:
         c.wait_send()
+    for c in outs:
+        c.wait()
 
 
 def step(args):
@@ -540,7 +590,7 @@
         step_kernel,
         out_shape=jax.ShapeDtypeStruct((8, HALF, 256), BF16),
         in_specs=[hbm] * len(args),
-        out_specs=pl.BlockSpec(memory_space=pltpu.VMEM),
+        out_specs=hbm,
         scratch_shapes=[
             vm((BAT, NOBS, MEMBERS), BF16),
             vm((BAT, NOBS), BF16),
@@ -577,12 +627,14 @@
             vm((4, 256, 256), F32),
             vm((4, 256, 256), BF16),
             vm((4, 256, 256), F32),
-            vm((24, 256, 256), BF16),
+            vm((24, 272, 256), BF16),
+            vm((24, 144, 256), BF16),
             vm((4, 4, HALF, 256), BF16),
             vm((4, 64, HALF), BF16),
             vm((24, 4, 256, 256), BF16),
             vm((4, 8, 256), F32),
-            vm((4, 256, 256), F32),
+            vm((4, 272, 256), F32),
+            vm((8, HALF, 256), BF16),
             pltpu.SemaphoreType.DMA((11,)),
             pltpu.SemaphoreType.DMA((BAT // GROUP,)),
             pltpu.SemaphoreType.DMA((4, 8)),

time: 69.3 us -> 66.2 us (0.955)
  Pallas kernels: 67.3 us -> 64.1 us
    pallas_call x1, Pallas kernels: 67.3 us -> 64.1 us  [step(): pl.pallas_call(step_kernel, out_shape=jax.ShapeDtypeStruct((8, HALF, 256)...]
where the time goes in v2:
time: 66.2 us; the launch traced here: 66 us
  Pallas kernels  64.1 us (97%)
  local copies, waits for them, and re-layouts  1.87 us (3%)
    pallas_call x1, Pallas kernels, step(): pl.pallas_call(step_kernel, out_shape=jax.ShapeDtypeStruct((8, HALF, 256)...  64.1 us
    unnamed x1, local copies, waits for them, and re-layouts  1.87 us

profile of v2, /device:TPU:1, one launch (start us, length us, event | category | flops | bytes accessed | tf_op | source)
XLA Modules:
  0.0 66.0 jit_solution(8667148364935273752)
XLA Ops:
  0.0 64.1 %step.1 = bf16[8,128,256]{2,1,0:T(8,128)(2,1)} custom-call(s32[1,32]{1,0:T(1,128)} %bitcast.6, s32[3,32]{1,0:T(4,128)} %bitcast.4, s32[1,32]{1,0:T(1,128)} %bitcast.7, s32[1,32]{1,0:T(1,128)} %len_h.1, bf16[32,512]{1,0:T(8,128)(2,1)} %weight_h.1, bf16[32,512]{1,0:T(8,128)(2,1)} %innov_h.1, bf16[3,32]{1,0:T(4,128)(2,1)} %bitcast.5, ...), custom_call_target="tpu_custom_call" | custom-call | tf_op jit(solution)/shard_map/step/pallas_call | solution.py:589
  64.2 1.9 %copy.13 = bf16[8,128,256]{2,1,0:T(8,128)(2,1)} copy(bf16[8,128,256]{2,1,0:T(8,128)(2,1)} %step.1) | data formatting | bytes 1048576

commit v3 on v2

--- a/solution.py
+++ b/solution.py
@@ -15,8 +15,8 @@
 MESH = pl.DeviceIdType.MESH
 F32 = jnp.float32
 BF16 = jnp.bfloat16
-COPIES = 64
-GROUP = 4
+COPIES = 60
+GROUP = 8
 CENTRE = MEMBERS - 1
 
 
@@ -451,8 +451,6 @@
             side[2 * a + j].wait_recv()
             column = 5 - 5 * j
             rim(a, (lead[a] + 1) * 6 + column, column)
-        for column in (0, 5):
-            unfold((lead[a] + 1) * 6 + column)
 
     def gather(slots, start=False):
         for t in range(4):
@@ -494,12 +492,8 @@
             scales.append(scale)
         for k in range(ITERS):
             scal = root_iteration(e_s, eb_s, z_s, scal, k)
-            if g == 1 and k in (2, 3):
-                corners_on(k - 2)
-            if g == 1 and k == 3:
-                for c in used[early:late]:
-                    c.wait_send()
-                gather([6 * r + c for r in (1, 2) for c in (0, 1, 4, 5)], start=True)
+        if g == 1:
+            corners_on(0)
         big = iota((256, 256), 0) == iota((256, 256), 1)
         tail16 = iota((16, 256), 0)
         turns = []
@@ -547,7 +541,12 @@
                 side.append(push(rims.at[slot], across, west if j == 0 else east))
             rim(a, slot, column)
 
-    gather([6 * r + c for r in (1, 2) for c in (2, 3)])
+    corners_on(1)
+    for n in (6, 11, 12, 17):
+        unfold(n)
+    gather([6 * r + c for r in (1, 2) for c in range(6)], start=True)
+    for c in used[early:late]:
+        c.wait_send()
     for column, c in inside:
         c.wait_recv()
     near, far = 18 * (1 - odd), 18 * odd

time: 66.2 us -> 63.3 us (0.956)
  Pallas kernels: 64.1 us -> 61.3 us
    pallas_call x1, Pallas kernels: 64.1 us -> 61.3 us  [step(): pl.pallas_call(step_kernel, out_shape=jax.ShapeDtypeStruct((8, HALF, 256)...]
where the time goes in v3:
time: 63.3 us; the launch traced here: 63.2 us
  Pallas kernels  61.3 us (97%)
  local copies, waits for them, and re-layouts  1.87 us (3%)
    pallas_call x1, Pallas kernels, step(): pl.pallas_call(step_kernel, out_shape=jax.ShapeDtypeStruct((8, HALF, 256)...  61.3 us
    unnamed x1, local copies, waits for them, and re-layouts  1.87 us

profile of v3, /device:TPU:1, one launch (start us, length us, event | category | flops | bytes accessed | tf_op | source)
XLA Modules:
  0.0 63.2 jit_solution(616426965171706879)
XLA Ops:
  0.0 61.3 %step.1 = bf16[8,128,256]{2,1,0:T(8,128)(2,1)} custom-call(s32[1,32]{1,0:T(1,128)} %bitcast.6, s32[3,32]{1,0:T(4,128)} %bitcast.4, s32[1,32]{1,0:T(1,128)} %bitcast.7, s32[1,32]{1,0:T(1,128)} %len_h.1, bf16[32,512]{1,0:T(8,128)(2,1)} %weight_h.1, bf16[32,512]{1,0:T(8,128)(2,1)} %innov_h.1, bf16[3,32]{1,0:T(4,128)(2,1)} %bitcast.5, ...), custom_call_target="tpu_custom_call" | custom-call | tf_op jit(solution)/shard_map/step/pallas_call | solution.py:588
  61.3 1.9 %copy.13 = bf16[8,128,256]{2,1,0:T(8,128)(2,1)} copy(bf16[8,128,256]{2,1,0:T(8,128)(2,1)} %step.1) | data formatting | bytes 1048576
